TPU v7x, 32 devices: a whole 2x2x4 slice. The times are simulated.
32 devices in a mesh: rep: 4 (over x, y), pp: 8 (over z, core).
Axes of the slice: x: 2, y: 2, z: 4, core: 2. Of those that a mesh axis runs over, the one named last changes fastest.
Arguments:
- x: bfloat16 [64, 512, 512], P('rep'), parts along dimension 0
- dy: bfloat16 [64, 512, 512], P('rep'), parts along dimension 0
- w_gate: bfloat16 [8, 512, 1408], P('pp')
- w_up: bfloat16 [8, 512, 1408], P('pp')
- w_down: bfloat16 [8, 1408, 512], P('pp')
Outputs:
- output 1: bfloat16 [32, 512, 1408], P(('rep', 'pp')), parts along dimension 0
- output 2: bfloat16 [32, 512, 1408], P(('rep', 'pp')), parts along dimension 0
- output 3: bfloat16 [32, 1408, 512], P(('rep', 'pp')), parts along dimension 0
There are 4 independent parts. A program takes and returns all parts, laid end to end along the dimension named above; an argument that names none is the same for every part.
All inputs are finite; a program needn't handle non-finite values.
Results may differ from a plain program's by a relative error of at most 0.0262.
Values are sent between devices in bfloat16 or wider.
A program may use at most 2 GiB of HBM per device.

v0:
```python
import jax
import jax.numpy as jnp
from jax import lax
from jax.sharding import PartitionSpec as P

NAMES = ("w_gate", "w_up", "w_down")


def matmul(a, w):
    return jnp.dot(a, w, preferred_element_type=jnp.float32).astype(jnp.bfloat16)


def normed(h):
    wide = h.astype(jnp.float32)
    scale = lax.rsqrt(jnp.mean(wide**2, -1, keepdims=True) + 1e-6)
    return (wide * scale).astype(jnp.bfloat16)


def layer(h, w):
    a = normed(h)
    gate = jnp.dot(a, w["w_gate"], preferred_element_type=jnp.float32)
    up = jnp.dot(a, w["w_up"], preferred_element_type=jnp.float32)
    return h + matmul((jax.nn.silu(gate) * up).astype(jnp.bfloat16), w["w_down"])


def stage(weights, h):
    for number in range(weights["w_gate"].shape[0]):
        h = layer(h, {name: w[number] for name, w in weights.items()})
    return h


def solution(mesh):
    stages = mesh.shape["pp"]
    onward = [(i, i + 1) for i in range(stages - 1)]
    back_again = [(i + 1, i) for i in range(stages - 1)]

    def step(x, dy, *arrays):
        weights = dict(zip(NAMES, arrays, strict=True))
        micro, me = x.shape[0], lax.axis_index("pp")
        kept, came = jnp.zeros_like(x), jnp.zeros_like(x[0])
        for t in range(micro + stages - 1):
            number = jnp.clip(t - me, 0, micro - 1)
            at_work = (t >= me) & (t - me < micro)
            h = jnp.where(me == 0, x[min(t, micro - 1)], came)
            was = lax.dynamic_index_in_dim(kept, number, 0, keepdims=False)
            kept = lax.dynamic_update_index_in_dim(kept, jnp.where(at_work, h, was), number, 0)
            came = lax.ppermute(stage(weights, h), "pp", onward)
        total = {name: jnp.zeros(w.shape, jnp.float32) for name, w in weights.items()}
        came, behind = jnp.zeros_like(x[0]), stages - 1 - me
        for t in range(micro + stages - 1):
            number = jnp.clip(t - behind, 0, micro - 1)
            at_work = (t >= behind) & (t - behind < micro)
            by_y = jnp.where(behind == 0, dy[min(t, micro - 1)], came)
            _, back = jax.vjp(stage, weights, lax.dynamic_index_in_dim(kept, number, 0, keepdims=False))
            by_w, by_h = back(by_y)
            total = {name: total[name] + jnp.where(at_work, by_w[name].astype(jnp.float32), 0.0) for name in NAMES}
            came = lax.ppermute(by_h, "pp", back_again)
        return tuple(total[name].astype(jnp.bfloat16) for name in NAMES)

    return jax.shard_map(
        step,
        mesh=mesh,
        in_specs=(P("rep", None, None),) * 2 + (P("pp", None, None),) * 3,
        out_specs=(P(("rep", "pp"), None, None),) * 3,
        check_vma=False,
    )
```

profile of v0, /device:TPU:1, one launch (start us, length us, event | category | flops | bytes accessed | tf_op | source)
XLA Modules:
  0.0 1028.7 jit_solution(8238046729641770596)
XLA Ops:
  15.7 6.1 collective-permute-done
  25.7 5.4 fusion.1034
  35.5 6.1 collective-permute-done.1
  45.5 5.3 fusion.1031
  55.2 6.1 collective-permute-done.2
  66.0 5.6 fusion.1028
  76.5 5.6 collective-permute-done.3
  86.8 5.6 fusion.1025
  96.8 6.1 collective-permute-done.4
  107.6 5.6 fusion.1022
  117.6 6.1 collective-permute-done.5
  128.4 5.6 fusion.1019
  138.4 6.1 collective-permute-done.6
  149.2 5.6 fusion.1016
  159.4 5.9 collective-permute-done.7
  170.0 5.6 fusion.1013
  180.0 6.1 collective-permute-done.8
  190.8 5.6 fusion.1010
  200.8 6.0 collective-permute-done.9
  274.2 5.3 fusion.998
  294.9 5.3 fusion.995
  377.5 5.3 fusion.983
  439.5 5.3 fusion.974
  1003.7 24.6 %fusion.305 = bf16[1,1408,512]{2,1,0:T(8,128)(2,1)} fusion(f32[1408,512]{1,0:T(8,128)} %fusion.68, f32[1408,512]{1,0:T(8,128)} %fusion.66, f32[1408,512]{1,0:T(8,128)} %fusion.64, f32[1408,512]{1,0:T(8,128)} %fusion.62, f32[1408,512]{1,0:T(8,128)} %fusion.60, f32[1408,512]{1,0:T(8,128)} %fusion.58, f32[1408,512]{1,0:T(8,128)} %fusion.56, ...), kind=kOutput, calls=%fused_computation.531 | convolution fusion | flops 761266176 | bytes 71172096 | tf_op jit(solution)/shard_map/transpose(jvp())/dot_general | solution.py:10
  (570 shorter events, 869.4 us)
Async XLA Ops:
  11.1 10.7 %collective-permute-start = (bf16[512,512]{1,0:T(8,128)(2,1)}, bf16[512,512]{1,0:T(8,128)(2,1)S(1)}, u32[]{:S(2)}, u32[]{:S(2)}) collective-permute-start(bf16[512,512]{1,0:T(8,128)(2,1)} %fusion.1037), channel_id=1, source_target_pairs={{0,1},{1,2},{2,3},{3,4},{4,5},{5,6},{6,7},{8,9},{9,10},{10,11},{11... | collective-permute-start | bytes 1572872 | tf_op jit(solution)/shard_map/ppermute | solution.py:47
  217.0 13.7 %collective-permute-start.10 = (bf16[512,512]{1,0:T(8,128)(2,1)}, bf16[512,512]{1,0:T(8,128)(2,1)S(1)}, u32[]{:S(2)}, u32[]{:S(2)}) collective-permute-start(bf16[512,512]{1,0:T(8,128)(2,1)} %fusion.1007), channel_id=1, source_target_pairs={{0,1},{1,2},{2,3},{3,4},{4,5},{5,6},{6,7},{8,9},{9,10},{10,11},{11... | collective-permute-start | bytes 1572872 | tf_op jit(solution)/shard_map/ppermute | solution.py:47
  258.8 10.6 %collective-permute-start.12 = (bf16[512,512]{1,0:T(8,128)(2,1)}, bf16[512,512]{1,0:T(8,128)(2,1)S(1)}, u32[]{:S(2)}, u32[]{:S(2)}) collective-permute-start(bf16[512,512]{1,0:T(8,128)(2,1)} %fusion.1001), channel_id=1, source_target_pairs={{0,1},{1,2},{2,3},{3,4},{4,5},{5,6},{6,7},{8,9},{9,10},{10,11},{11... | collective-permute-start | bytes 1572872 | tf_op jit(solution)/shard_map/ppermute | solution.py:47
  279.5 10.6 %collective-permute-start.13 = (bf16[512,512]{1,0:T(8,128)(2,1)}, bf16[512,512]{1,0:T(8,128)(2,1)S(1)}, u32[]{:S(2)}, u32[]{:S(2)}) collective-permute-start(bf16[512,512]{1,0:T(8,128)(2,1)} %fusion.998), channel_id=1, source_target_pairs={{0,1},{1,2},{2,3},{3,4},{4,5},{5,6},{6,7},{8,9},{9,10},{10,11},{11... | collective-permute-start | bytes 1572872 | tf_op jit(solution)/shard_map/ppermute | solution.py:47
  300.2 10.6 %collective-permute-start.14 = (bf16[512,512]{1,0:T(8,128)(2,1)}, bf16[512,512]{1,0:T(8,128)(2,1)S(1)}, u32[]{:S(2)}, u32[]{:S(2)}) collective-permute-start(bf16[512,512]{1,0:T(8,128)(2,1)} %fusion.995), channel_id=1, source_target_pairs={{0,1},{1,2},{2,3},{3,4},{4,5},{5,6},{6,7},{8,9},{9,10},{10,11},{11... | collective-permute-start | bytes 1572872 | tf_op jit(solution)/shard_map/ppermute | solution.py:47
  320.8 10.8 %collective-permute-start.15 = (bf16[512,512]{1,0:T(8,128)(2,1)}, bf16[512,512]{1,0:T(8,128)(2,1)S(1)}, u32[]{:S(2)}, u32[]{:S(2)}) collective-permute-start(bf16[512,512]{1,0:T(8,128)(2,1)} %fusion.992), channel_id=1, source_target_pairs={{0,1},{1,2},{2,3},{3,4},{4,5},{5,6},{6,7},{8,9},{9,10},{10,11},{11... | collective-permute-start | bytes 1572872 | tf_op jit(solution)/shard_map/ppermute | solution.py:47
  362.1 10.6 %collective-permute-start.17 = (bf16[512,512]{1,0:T(8,128)(2,1)}, bf16[512,512]{1,0:T(8,128)(2,1)S(1)}, u32[]{:S(2)}, u32[]{:S(2)}) collective-permute-start(bf16[512,512]{1,0:T(8,128)(2,1)} %fusion.986), channel_id=1, source_target_pairs={{0,1},{1,2},{2,3},{3,4},{4,5},{5,6},{6,7},{8,9},{9,10},{10,11},{11... | collective-permute-start | bytes 1572872 | tf_op jit(solution)/shard_map/ppermute | solution.py:47
  382.8 10.6 %collective-permute-start.18 = (bf16[512,512]{1,0:T(8,128)(2,1)}, bf16[512,512]{1,0:T(8,128)(2,1)S(1)}, u32[]{:S(2)}, u32[]{:S(2)}) collective-permute-start(bf16[512,512]{1,0:T(8,128)(2,1)} %fusion.983), channel_id=1, source_target_pairs={{0,1},{1,2},{2,3},{3,4},{4,5},{5,6},{6,7},{8,9},{9,10},{10,11},{11... | collective-permute-start | bytes 1572872 | tf_op jit(solution)/shard_map/ppermute | solution.py:47
  403.4 10.6 %collective-permute-start.19 = (bf16[512,512]{1,0:T(8,128)(2,1)}, bf16[512,512]{1,0:T(8,128)(2,1)S(1)}, u32[]{:S(2)}, u32[]{:S(2)}) collective-permute-start(bf16[512,512]{1,0:T(8,128)(2,1)} %fusion.980), channel_id=1, source_target_pairs={{0,1},{1,2},{2,3},{3,4},{4,5},{5,6},{6,7},{8,9},{9,10},{10,11},{11... | collective-permute-start | bytes 1572872 | tf_op jit(solution)/shard_map/ppermute | solution.py:47
  424.1 10.6 %collective-permute-start.20 = (bf16[512,512]{1,0:T(8,128)(2,1)}, bf16[512,512]{1,0:T(8,128)(2,1)S(1)}, u32[]{:S(2)}, u32[]{:S(2)}) collective-permute-start(bf16[512,512]{1,0:T(8,128)(2,1)} %fusion.977), channel_id=1, source_target_pairs={{0,1},{1,2},{2,3},{3,4},{4,5},{5,6},{6,7},{8,9},{9,10},{10,11},{11... | collective-permute-start | bytes 1572872 | tf_op jit(solution)/shard_map/ppermute | solution.py:47
  444.7 10.6 %collective-permute-start.21 = (bf16[512,512]{1,0:T(8,128)(2,1)}, bf16[512,512]{1,0:T(8,128)(2,1)S(1)}, u32[]{:S(2)}, u32[]{:S(2)}) collective-permute-start(bf16[512,512]{1,0:T(8,128)(2,1)} %fusion.974), channel_id=1, source_target_pairs={{0,1},{1,2},{2,3},{3,4},{4,5},{5,6},{6,7},{8,9},{9,10},{10,11},{11... | collective-permute-start | bytes 1572872 | tf_op jit(solution)/shard_map/ppermute | solution.py:47
  473.6 11.3 %collective-permute-start.22 = (bf16[512,512]{1,0:T(8,128)(2,1)S(1)}, bf16[512,512]{1,0:T(8,128)(2,1)S(1)}, u32[]{:S(2)}, u32[]{:S(2)}) collective-permute-start(bf16[512,512]{1,0:T(8,128)(2,1)S(1)} %fusion.1306), channel_id=1, source_target_pairs={{1,0},{2,1},{3,2},{4,3},{5,4},{6,5},{7,6},{9,8},{10,9},{11,10},{12... | collective-permute-start | bytes 1572872 | tf_op jit(solution)/shard_map/ppermute | solution.py:57
  493.7 10.5 %collective-permute-start.23 = (bf16[512,512]{1,0:T(8,128)(2,1)S(1)}, bf16[512,512]{1,0:T(8,128)(2,1)S(1)}, u32[]{:S(2)}, u32[]{:S(2)}) collective-permute-start(bf16[512,512]{1,0:T(8,128)(2,1)S(1)} %fusion.1305), channel_id=1, source_target_pairs={{1,0},{2,1},{3,2},{4,3},{5,4},{6,5},{7,6},{9,8},{10,9},{11,10},{12... | collective-permute-start | bytes 1572872 | tf_op jit(solution)/shard_map/ppermute | solution.py:57
  518.0 10.5 %collective-permute-start.24 = (bf16[512,512]{1,0:T(8,128)(2,1)S(1)}, bf16[512,512]{1,0:T(8,128)(2,1)S(1)}, u32[]{:S(2)}, u32[]{:S(2)}) collective-permute-start(bf16[512,512]{1,0:T(8,128)(2,1)S(1)} %fusion.1304), channel_id=1, source_target_pairs={{1,0},{2,1},{3,2},{4,3},{5,4},{6,5},{7,6},{9,8},{10,9},{11,10},{12... | collective-permute-start | bytes 1572872 | tf_op jit(solution)/shard_map/ppermute | solution.py:57
  542.4 10.5 %collective-permute-start.25 = (bf16[512,512]{1,0:T(8,128)(2,1)S(1)}, bf16[512,512]{1,0:T(8,128)(2,1)S(1)}, u32[]{:S(2)}, u32[]{:S(2)}) collective-permute-start(bf16[512,512]{1,0:T(8,128)(2,1)S(1)} %fusion.1303), channel_id=1, source_target_pairs={{1,0},{2,1},{3,2},{4,3},{5,4},{6,5},{7,6},{9,8},{10,9},{11,10},{12... | collective-permute-start | bytes 1572872 | tf_op jit(solution)/shard_map/ppermute | solution.py:57
  566.8 10.5 %collective-permute-start.26 = (bf16[512,512]{1,0:T(8,128)(2,1)S(1)}, bf16[512,512]{1,0:T(8,128)(2,1)S(1)}, u32[]{:S(2)}, u32[]{:S(2)}) collective-permute-start(bf16[512,512]{1,0:T(8,128)(2,1)S(1)} %fusion.1302), channel_id=1, source_target_pairs={{1,0},{2,1},{3,2},{4,3},{5,4},{6,5},{7,6},{9,8},{10,9},{11,10},{12... | collective-permute-start | bytes 1572872 | tf_op jit(solution)/shard_map/ppermute | solution.py:57
  591.2 10.5 %collective-permute-start.27 = (bf16[512,512]{1,0:T(8,128)(2,1)S(1)}, bf16[512,512]{1,0:T(8,128)(2,1)S(1)}, u32[]{:S(2)}, u32[]{:S(2)}) collective-permute-start(bf16[512,512]{1,0:T(8,128)(2,1)S(1)} %fusion.1301), channel_id=1, source_target_pairs={{1,0},{2,1},{3,2},{4,3},{5,4},{6,5},{7,6},{9,8},{10,9},{11,10},{12... | collective-permute-start | bytes 1572872 | tf_op jit(solution)/shard_map/ppermute | solution.py:57
  615.6 10.5 %collective-permute-start.28 = (bf16[512,512]{1,0:T(8,128)(2,1)S(1)}, bf16[512,512]{1,0:T(8,128)(2,1)S(1)}, u32[]{:S(2)}, u32[]{:S(2)}) collective-permute-start(bf16[512,512]{1,0:T(8,128)(2,1)S(1)} %fusion.1300), channel_id=1, source_target_pairs={{1,0},{2,1},{3,2},{4,3},{5,4},{6,5},{7,6},{9,8},{10,9},{11,10},{12... | collective-permute-start | bytes 1572872 | tf_op jit(solution)/shard_map/ppermute | solution.py:57
  640.0 10.5 %collective-permute-start.29 = (bf16[512,512]{1,0:T(8,128)(2,1)S(1)}, bf16[512,512]{1,0:T(8,128)(2,1)S(1)}, u32[]{:S(2)}, u32[]{:S(2)}) collective-permute-start(bf16[512,512]{1,0:T(8,128)(2,1)S(1)} %fusion.1299), channel_id=1, source_target_pairs={{1,0},{2,1},{3,2},{4,3},{5,4},{6,5},{7,6},{9,8},{10,9},{11,10},{12... | collective-permute-start | bytes 1572872 | tf_op jit(solution)/shard_map/ppermute | solution.py:57
  664.4 10.5 %collective-permute-start.30 = (bf16[512,512]{1,0:T(8,128)(2,1)S(1)}, bf16[512,512]{1,0:T(8,128)(2,1)S(1)}, u32[]{:S(2)}, u32[]{:S(2)}) collective-permute-start(bf16[512,512]{1,0:T(8,128)(2,1)S(1)} %fusion.1298), channel_id=1, source_target_pairs={{1,0},{2,1},{3,2},{4,3},{5,4},{6,5},{7,6},{9,8},{10,9},{11,10},{12... | collective-permute-start | bytes 1572872 | tf_op jit(solution)/shard_map/ppermute | solution.py:57
  688.8 10.5 %collective-permute-start.31 = (bf16[512,512]{1,0:T(8,128)(2,1)S(1)}, bf16[512,512]{1,0:T(8,128)(2,1)S(1)}, u32[]{:S(2)}, u32[]{:S(2)}) collective-permute-start(bf16[512,512]{1,0:T(8,128)(2,1)S(1)} %fusion.1297), channel_id=1, source_target_pairs={{1,0},{2,1},{3,2},{4,3},{5,4},{6,5},{7,6},{9,8},{10,9},{11,10},{12... | collective-permute-start | bytes 1572872 | tf_op jit(solution)/shard_map/ppermute | solution.py:57
  713.2 10.5 %collective-permute-start.32 = (bf16[512,512]{1,0:T(8,128)(2,1)S(1)}, bf16[512,512]{1,0:T(8,128)(2,1)S(1)}, u32[]{:S(2)}, u32[]{:S(2)}) collective-permute-start(bf16[512,512]{1,0:T(8,128)(2,1)S(1)} %fusion.1296), channel_id=1, source_target_pairs={{1,0},{2,1},{3,2},{4,3},{5,4},{6,5},{7,6},{9,8},{10,9},{11,10},{12... | collective-permute-start | bytes 1572872 | tf_op jit(solution)/shard_map/ppermute | solution.py:57
  737.6 10.5 %collective-permute-start.33 = (bf16[512,512]{1,0:T(8,128)(2,1)S(1)}, bf16[512,512]{1,0:T(8,128)(2,1)S(1)}, u32[]{:S(2)}, u32[]{:S(2)}) collective-permute-start(bf16[512,512]{1,0:T(8,128)(2,1)S(1)} %fusion.1295), channel_id=1, source_target_pairs={{1,0},{2,1},{3,2},{4,3},{5,4},{6,5},{7,6},{9,8},{10,9},{11,10},{12... | collective-permute-start | bytes 1572872 | tf_op jit(solution)/shard_map/ppermute | solution.py:57
  762.0 10.5 %collective-permute-start.34 = (bf16[512,512]{1,0:T(8,128)(2,1)S(1)}, bf16[512,512]{1,0:T(8,128)(2,1)S(1)}, u32[]{:S(2)}, u32[]{:S(2)}) collective-permute-start(bf16[512,512]{1,0:T(8,128)(2,1)S(1)} %fusion.1294), channel_id=1, source_target_pairs={{1,0},{2,1},{3,2},{4,3},{5,4},{6,5},{7,6},{9,8},{10,9},{11,10},{12... | collective-permute-start | bytes 1572872 | tf_op jit(solution)/shard_map/ppermute | solution.py:57
  (70 other events, 455.4 us)
where the time goes:
time: 1050 us; the launch traced here: 1030 us
  matrix products  584 us (56%)
  waiting for transfers between devices  148 us (14%)
  starting transfers between devices  145 us (14%)
  other arithmetic  97.6 us (9%)
  local copies, waits for them, and re-layouts  50.8 us (5%)
    dot_general x68, matrix products, matmul(): jnp.dot(a, w, preferred_element_type=jnp.float32).astype(jnp.bfloat16)  228 us
    dot_general x90, matrix products, layer(): gate = jnp.dot(a, w['w_gate'], preferred_element_type=jnp.float32)  197 us
    dot_general x68, matrix products, layer(): up = jnp.dot(a, w['w_up'], preferred_element_type=jnp.float32)  159 us
    ppermute x22, starting transfers between devices, step(): came = lax.ppermute(stage(weights, h), 'pp', onward)  97.1 us
    ppermute x22, waiting for transfers between devices, step(): came = lax.ppermute(by_h, 'pp', back_again)  84.5 us
    ppermute x22, waiting for transfers between devices, step(): came = lax.ppermute(stage(weights, h), 'pp', onward)  63.1 us
    ppermute x22, starting transfers between devices, step(): came = lax.ppermute(by_h, 'pp', back_again)  48.2 us
    dynamic_update_slice x23, other arithmetic, step(): lax.dynamic_update_index_in_dim(kept, jnp.where(at_work, h, was), number, 0)  35.3 us
  transfers between devices with their start and end apart: 44, of which 41 were waited for; matrix products, arithmetic and copies ran while one was open for 17% of the time, Pallas kernels for 0%

commit v1 on v0

v1 whole, which is shorter than its diff:
```python
import functools

import jax
import jax.numpy as jnp
from jax import lax
from jax.experimental import pallas as pl
from jax.experimental.pallas import tpu as pltpu
from jax.sharding import PartitionSpec as P

F32, BF16 = jnp.float32, jnp.bfloat16
CHUNKS = 2
SLOTS = 4
LAG = 1
WARM = (10, 9, 7, 6, 4, 3, 1, 0)
TILE = 256


def dot(a, b):
    return jnp.dot(a, b, preferred_element_type=F32)


def columns(ff):
    full, rest = divmod(ff, TILE)
    out = [(j * TILE, ff + rest + j * TILE, TILE) for j in range(full)]
    if rest:
        out.append((full * TILE, ff, rest))
    return out


def kernel(cfg, x_ref, dy_ref, wg_ref, wu_ref, wd_ref, og_ref, ou_ref, od_ref, hin, din, wgu, wgut, wd, wdt, acc_gu, acc_d, hout, bout,
           dgu, hid, abuf, at, dyt, hidf, fsem, bsem, fsend, bsend, wsem, osem):
    micro, tokens, d, ff, stages, warms = cfg
    chunks, slots = CHUNKS, SLOTS
    rows = tokens // chunks
    full, rest = divmod(ff, TILE)
    body = full * TILE
    me = lax.axis_index("pp")
    last = stages - 1

    def up_parts():
        parts = [((0, body), (ff + rest, body))]
        if rest:
            parts.append(((body, rest), (ff, rest)))
        return parts

    loads = [pltpu.make_async_copy(wg_ref.at[0], wgu.at[:, pl.ds(0, ff)], wsem.at[0])]
    for n, (src, dst) in enumerate(up_parts()):
        loads.append(pltpu.make_async_copy(wu_ref.at[0, :, pl.ds(*src)], wgu.at[:, pl.ds(*dst)], wsem.at[1 + n]))
    loads.append(pltpu.make_async_copy(wd_ref.at[0], wd, wsem.at[3]))

    def h_in(m, c):
        r = pl.ds(pl.multiple_of(c * rows, rows), rows)
        return pltpu.make_async_copy(x_ref.at[m, r], hin.at[m, r], fsem.at[m, c])

    def d_in(m, c):
        r = pl.ds(pl.multiple_of(c * rows, rows), rows)
        return pltpu.make_async_copy(dy_ref.at[m, r], din.at[m, r], bsem.at[m, c])

    def each(make):
        def go(n, _):
            make(n // chunks, lax.rem(n, chunks)).start()
            return 0

        lax.fori_loop(0, micro * chunks, go, 0)

    @pl.when(me == 0)
    def _():
        h_in(0, 0).start()

    for copy in loads:
        copy.start()

    @pl.when(me == 0)
    def _():
        def go(n, _):
            h_in(n // chunks, lax.rem(n, chunks)).start()
            return 0

        lax.fori_loop(1, micro * chunks, go, 0)

    @pl.when(me == last)
    def _():
        each(d_in)

    barrier = pltpu.get_barrier_semaphore()

    @pl.when(me > 0)
    def _():
        pl.semaphore_signal(barrier, inc=1, device_id={"pp": me - 1})

    @pl.when(me < last)
    def _():
        pl.semaphore_signal(barrier, inc=1, device_id={"pp": me + 1})

    @pl.when((me > 0) & (me < last))
    def _():
        pl.semaphore_wait(barrier, 2)

    @pl.when((me == 0) | (me == last))
    def _():
        pl.semaphore_wait(barrier, 1)

    for copy in loads:
        copy.wait()

    def f_send(m, c):
        r = pl.ds(pl.multiple_of(c * rows, rows), rows)
        s = lax.rem(m, slots)
        return pltpu.make_async_remote_copy(
            src_ref=hout.at[s, r], dst_ref=hin.at[m, r], send_sem=fsend.at[s, c], recv_sem=fsem.at[m, c], device_id={"pp": me + 1})

    def b_send(m, c):
        r = pl.ds(pl.multiple_of(c * rows, rows), rows)
        s = lax.rem(m, slots)
        return pltpu.make_async_remote_copy(
            src_ref=bout.at[s, r], dst_ref=din.at[m, r], send_sem=bsend.at[s, c], recv_sem=bsem.at[m, c], device_id={"pp": me - 1})

    def scale_of(wide):
        return lax.rsqrt(jnp.mean(wide * wide, -1, keepdims=True) + 1e-6)

    def forward(m):
        def piece(c, _):
            r = pl.ds(pl.multiple_of(c * rows, rows), rows)
            h_in(m, c).wait()

            @pl.when(m >= slots)
            def _():
                f_send(m - slots, c).wait_send()

            h = hin[m, r]
            wide = h.astype(F32)
            a = (wide * scale_of(wide)).astype(BF16)
            for g0, u0, w in columns(ff):
                if w == TILE:
                    g, u = dot(a, wgu[:, g0:g0 + w]), dot(a, wgu[:, u0:u0 + w])
                else:
                    gu = dot(a, wgu[:, g0:g0 + 2 * w])
                    g, u = gu[:, :w], gu[:, w:]
                hidf[:, g0:g0 + w] = (g * lax.logistic(g) * u).astype(BF16)
            hout[lax.rem(m, slots), r] = h + dot(hidf[...], wd[...]).astype(BF16)
            f_send(m, c).start()
            return 0

        lax.fori_loop(0, chunks, piece, 0)

    def backward(m):
        s = lax.rem(m, LAG + 1)

        def piece(c, _):
            r = pl.ds(pl.multiple_of(c * rows, rows), rows)

            @pl.when(me == last)
            def _():
                h_in(m, c).wait()

            d_in(m, c).wait()

            h = hin[m, r]
            wide = h.astype(F32)
            a = (wide * scale_of(wide)).astype(BF16)
            abuf[s, r] = a
            by_y = din[m, r]
            for g0, u0, w in columns(ff):
                if w == TILE:
                    g, u = dot(a, wgu[:, g0:g0 + w]), dot(a, wgu[:, u0:u0 + w])
                else:
                    gu = dot(a, wgu[:, g0:g0 + 2 * w])
                    g, u = gu[:, :w], gu[:, w:]
                by_z = dot(by_y, wdt[:, g0:g0 + w]).astype(BF16).astype(F32)
                sig = lax.logistic(g)
                silu = g * sig
                hid[s, r, g0:g0 + w] = (silu * u).astype(BF16)
                dgu[s, r, g0:g0 + w] = (by_z * u * (sig + silu * (1.0 - sig))).astype(BF16)
                dgu[s, r, u0:u0 + w] = (by_z * silu).astype(BF16)

            @pl.when(me > 0)
            def _():
                @pl.when(m >= slots)
                def _():
                    b_send(m - slots, c).wait_send()

                by_a = dot(dgu[s, r, :ff], wgut[:ff]).astype(BF16) + dot(dgu[s, r, ff:], wgut[ff:]).astype(BF16)
                by_a = by_a.astype(F32)
                wide = hin[m, r].astype(F32)
                scale = scale_of(wide)
                by_scale = jnp.sum(by_a * wide, -1, keepdims=True)
                by_wide = by_a * scale - wide * (by_scale * scale * scale * scale * (1.0 / d))
                bout[lax.rem(m, slots), r] = din[m, r] + by_wide.astype(BF16)
                b_send(m, c).start()

            return 0

        lax.fori_loop(0, chunks, piece, 0)

    def gradients(m):
        s = lax.rem(m, LAG + 1)
        at[...] = abuf[s].T
        dyt[...] = din[m].T
        for n in range(0, 2 * ff, TILE):
            w = min(TILE, 2 * ff - n)
            acc_gu[:, n:n + w] += dot(at[...], dgu[s, :, n:n + w]).astype(BF16).astype(F32)
        for n in range(0, ff, TILE):
            w = min(TILE, ff - n)
            acc_d[:, n:n + w] += dot(dyt[...], hid[s, :, n:n + w]).astype(BF16).astype(F32)

    warm = sum(jnp.where(me == n, w, 0) for n, w in enumerate(warms))
    start = jnp.where(me == 0, 0, -1)

    def tick(i, _):
        @pl.when((i >= 0) & (i < micro) & (me < last))
        def _():
            forward(i)

        @pl.when(i == start)
        def _():
            wdt[...] = wd[...].T
            for n in range(0, 2 * ff, TILE):
                w = min(TILE, 2 * ff - n)
                wgut[n:n + w] = wgu[:, n:n + w].T
            acc_gu[...] = jnp.zeros_like(acc_gu)
            acc_d[...] = jnp.zeros_like(acc_d)

        b = i - warm

        @pl.when((b >= 0) & (b < micro))
        def _():
            backward(b)

        @pl.when((b >= LAG) & (b < micro + LAG))
        def _():
            gradients(b - LAG)

        return 0

    lax.fori_loop(start, micro + warm + LAG, tick, 0)

    out_gu, out_d = dgu.at[0], wd
    stores = []
    out_gu[:, :ff] = acc_gu[:, :ff].astype(BF16)
    stores.append(pltpu.make_async_copy(out_gu.at[:, pl.ds(0, ff)], og_ref.at[0], osem.at[0]))
    stores[-1].start()
    out_gu[:, ff:] = acc_gu[:, ff:].astype(BF16)
    for n, (dst, src) in enumerate(up_parts()):
        stores.append(pltpu.make_async_copy(out_gu.at[:, pl.ds(*src)], ou_ref.at[0, :, pl.ds(*dst)], osem.at[1 + n]))
        stores[-1].start()
    out_d[...] = acc_d[...].astype(BF16).T
    stores.append(pltpu.make_async_copy(out_d, od_ref.at[0], osem.at[3]))
    stores[-1].start()

    def drain(send):
        def go(n, _):
            send(micro - slots + n // chunks, lax.rem(n, chunks)).wait_send()
            return 0

        lax.fori_loop(0, slots * chunks, go, 0)

    @pl.when(me < last)
    def _():
        drain(f_send)

    @pl.when(me > 0)
    def _():
        drain(b_send)

    for copy in stores:
        copy.wait()


def solution(mesh):
    stages = mesh.shape["pp"]

    def step(x, dy, wg, wu, wd):
        micro, tokens, d = x.shape
        ff = wg.shape[-1]
        cfg = (micro, tokens, d, ff, stages, WARM[:stages] if stages == len(WARM) else tuple(stages - 1 - n for n in range(stages)))
        hbm = pl.BlockSpec(memory_space=pl.ANY)
        keep = LAG + 1
        flops = 2 * micro * tokens * d * ff * 11
        return pl.pallas_call(
            functools.partial(kernel, cfg),
            out_shape=(
                jax.ShapeDtypeStruct((1, d, ff), BF16),
                jax.ShapeDtypeStruct((1, d, ff), BF16),
                jax.ShapeDtypeStruct((1, ff, d), BF16),
            ),
            in_specs=[hbm] * 5,
            out_specs=(hbm,) * 3,
            scratch_shapes=[
                pltpu.VMEM((micro, tokens, d), BF16),
                pltpu.VMEM((micro, tokens, d), BF16),
                pltpu.VMEM((d, 2 * ff), BF16),
                pltpu.VMEM((2 * ff, d), BF16),
                pltpu.VMEM((ff, d), BF16),
                pltpu.VMEM((d, ff), BF16),
                pltpu.VMEM((d, 2 * ff), F32),
                pltpu.VMEM((d, ff), F32),
                pltpu.VMEM((SLOTS, tokens, d), BF16),
                pltpu.VMEM((SLOTS, tokens, d), BF16),
                pltpu.VMEM((keep, tokens, 2 * ff), BF16),
                pltpu.VMEM((keep, tokens, ff), BF16),
                pltpu.VMEM((keep, tokens, d), BF16),
                pltpu.VMEM((d, tokens), BF16),
                pltpu.VMEM((d, tokens), BF16),
                pltpu.VMEM((tokens // CHUNKS, ff), BF16),
                pltpu.SemaphoreType.DMA((micro, CHUNKS)),
                pltpu.SemaphoreType.DMA((micro, CHUNKS)),
                pltpu.SemaphoreType.DMA((SLOTS, CHUNKS)),
                pltpu.SemaphoreType.DMA((SLOTS, CHUNKS)),
                pltpu.SemaphoreType.DMA((4,)),
                pltpu.SemaphoreType.DMA((4,)),
            ],
            compiler_params=pltpu.CompilerParams(collective_id=0, has_side_effects=True, vmem_limit_bytes=67_000_000),
            cost_estimate=pl.CostEstimate(flops=flops, bytes_accessed=40_000_000, transcendentals=0),
            name="pipeline",
        )(x, dy, wg, wu, wd)

    return jax.shard_map(
        step,
        mesh=mesh,
        in_specs=(P("rep", None, None),) * 2 + (P("pp", None, None),) * 3,
        out_specs=(P(("rep", "pp"), None, None),) * 3,
        check_vma=False,
    )
```

time: 1050 us -> 244 us (0.23)
  the two profiles are of different devices: /device:TPU:1 before, /device:TPU:2 now
where the time goes in v1:
time: 244 us
  Pallas kernels  238 us (98%)
  local copies, waits for them, and re-layouts  5.66 us (2%)
    pallas_call x1, Pallas kernels, step(): pl.pallas_call(functools.partial(kernel, cfg), out_shape=(jax.ShapeDtypeS...  238 us
    unnamed x7, local copies, waits for them, and re-layouts  5.66 us

profile of v1, /device:TPU:2, one launch (start us, length us, event | category | flops | bytes accessed | tf_op | source)
XLA Modules:
  0.0 244.3 jit_solution(3504183367534176184)
XLA Ops:
  0.6 238.0 %pipeline.1 = (bf16[1,512,1408]{2,1,0:T(8,128)(2,1)}, bf16[1,512,1408]{2,1,0:T(8,128)(2,1)}, bf16[1,1408,512]{2,1,0:T(8,128)(2,1)}) custom-call(bf16[16,512,512]{2,1,0:T(8,128)(2,1)} %x_ref.1, bf16[16,512,512]{2,1,0:T(8,128)(2,1)} %dy_ref.1, bf16[1,512,1408]{2,1,0:T(8,128)(2,1)} %wg_ref.1, bf16[1,512,1408]{2,1,0:T(8,128)(2,1)} %wu_ref.1, ...), custom_call_target="tpu_custom_call" | custom-call | flops 129922760704 | bytes 40000000 | tf_op jit(solution)/shard_map/pipeline/pallas_call | solution.py:279
  238.6 0.0 copy-start.1
  238.6 2.7 %copy.11 = bf16[1,512,1408]{2,1,0:T(8,128)(2,1)} copy(bf16[1,512,1408]{2,1,0:T(8,128)(2,1)} %get-tuple-element.6) | data formatting | bytes 2883584
  241.3 0.0 copy-done.1
  241.3 0.0 copy-start
  241.3 1.1 copy.12
  242.4 0.8 copy-done
  243.2 1.1 copy.13
Async XLA Ops:
  238.6 2.7 %copy-start.1 = (bf16[1,512,1408]{2,1,0:T(8,128)(2,1)S(1)}, bf16[1,512,1408]{2,1,0:T(8,128)(2,1)}, u32[]{:S(2)}) copy-start(bf16[1,512,1408]{2,1,0:T(8,128)(2,1)} %get-tuple-element.7) | copy-start | bytes 4325380
  241.3 1.9 copy-start

commit v2 on v1

v2 whole, which is shorter than its diff:
```python
import functools

import jax
import jax.numpy as jnp
from jax import lax
from jax.experimental import pallas as pl
from jax.experimental.pallas import tpu as pltpu
from jax.sharding import PartitionSpec as P

F32, BF16 = jnp.float32, jnp.bfloat16
CHUNKS, FINE = 2, 4
FIRST, FINAL = 1, 1
SLOTS = 2
ORDER = (
    "FTFFFFFFFFFFFFFBFBFWBBWBWWBBWBWBWBWBWBWBWBWWBBWWW",
    "TFFFFFFFFFFFFFBFBFWBFBWBWWBBWBWBWBWBWBWBWBWWBBWWW",
    "TFFFFFFBFFFFBFFWFBFBFBFBWBWBWBWBWBWBWBWBWWBBWWWWW",
    "TFFFFFBFFFFBFWFFBFBFBFBFBWBWBWBWBWBWBWBWWBBWWWWWW",
    "TFFFBFFFBFWFBFFBFBFBFBFBFBFBBWWBWBWBWWBBWWWWWWWWW",
    "TFFBFFFBFWBFFBFBFBFBFBFBFBFBFBWBWBWWBBWWWWWWWWWWW",
    "TFBFBFWFBFWBFBFBFBFBFBFBFBFBFBFBFBBWWWWWWWWWWWWWW",
    "TBBBWBBWBBWBBWBBWBBWBBBWWWWWWWWWW",
)
TILE = 256


def packed(order):
    codes = ["TFBW".index(step) for step in order]
    return [sum(code * 4**n for n, code in enumerate(codes[k:k + 15])) for k in range(0, len(codes), 15)]


def dot(a, b):
    return jnp.dot(a, b, preferred_element_type=F32)


def columns(ff):
    full, rest = divmod(ff, TILE)
    out = [(j * TILE, ff + rest + j * TILE, TILE) for j in range(full)]
    if rest:
        out.append((full * TILE, ff, rest))
    return out


def scale_of(wide):
    return lax.rsqrt(jnp.mean(wide * wide, -1, keepdims=True) + 1e-6)


def normed(h):
    wide = h.astype(F32)
    return (wide * scale_of(wide)).astype(BF16)


def kernel(cfg, x_ref, dy_ref, wg_ref, wu_ref, wd_ref, og_ref, ou_ref, od_ref, pq_hbm, hid_hbm, dgu_hbm, hin, din, wgu, wgut, wd, wdt, acc_gu, acc_d, hout, bout,
           at, dyt, hidf, fst, bst, gst, wgin, whin, fsem, bsem, fsend, bsend, fss, hss, bss, gss, ws, wsem, osem):
    micro, tokens, d, ff, stages, orders = cfg
    unit = tokens // FINE
    full, rest = divmod(ff, TILE)
    body = full * TILE
    me = lax.axis_index("pp")
    last = stages - 1

    def by_stage(table):
        return sum(jnp.where(me == n, w, 0) for n, w in enumerate(table))

    words = [packed(order) for order in orders]
    steps = by_stage([len(order) for order in orders])

    def code(k):
        word = sum(jnp.where(k // 15 == j, by_stage([w[j] if j < len(w) else 0 for w in words]), 0) for j in range(max(map(len, words))))
        return (word // sum(jnp.where(k % 15 == j, 4**j, 0) for j in range(15))) % 4

    def is_fine(m):
        return (m < FIRST) | (m >= micro - FINAL)

    def sized(m, go):
        @pl.when(is_fine(m))
        def _():
            go(unit, FINE)

        @pl.when(jnp.logical_not(is_fine(m)))
        def _():
            go(tokens // CHUNKS, CHUNKS)

    def up_parts():
        parts = [((0, body), (ff + rest, body))]
        if rest:
            parts.append(((body, rest), (ff, rest)))
        return parts

    def span(c, rows):
        return pl.ds(pl.multiple_of(c * rows, rows), rows)

    def first_of(c, rows):
        return c * (rows // unit)

    def h_in(m, c, rows):
        r = span(c, rows)
        return pltpu.make_async_copy(x_ref.at[m, r], hin.at[m, r], fsem.at[m, first_of(c, rows)])

    def d_in(m, c, rows):
        r = span(c, rows)
        return pltpu.make_async_copy(dy_ref.at[m, r], din.at[m, r], bsem.at[m, first_of(c, rows)])

    def f_send(m, c, rows):
        r, s = span(c, rows), lax.rem(m, SLOTS)
        return pltpu.make_async_remote_copy(
            src_ref=hout.at[s, r], dst_ref=hin.at[m, r], send_sem=fsend.at[s, first_of(c, rows)], recv_sem=fsem.at[m, first_of(c, rows)],
            device_id={"pp": me + 1})

    def b_send(m, c, rows):
        r, s = span(c, rows), lax.rem(m, SLOTS)
        return pltpu.make_async_remote_copy(
            src_ref=bout.at[s, r], dst_ref=din.at[m, r], send_sem=bsend.at[s, first_of(c, rows)], recv_sem=bsem.at[m, first_of(c, rows)],
            device_id={"pp": me - 1})

    def keep_pq(m, c, rows):
        p = lax.rem(c, 2)
        return pltpu.make_async_copy(fst.at[p, pl.ds(0, rows)], pq_hbm.at[m, span(c, rows)], fss.at[p])

    def keep_hid(m, c, rows):
        p = lax.rem(c, 2)
        return pltpu.make_async_copy(hidf.at[p, pl.ds(0, rows)], hid_hbm.at[m, span(c, rows)], hss.at[p])

    def keep_dgu(m, c, rows):
        p = lax.rem(c, 2)
        return pltpu.make_async_copy(gst.at[p, pl.ds(0, rows)], dgu_hbm.at[m, span(c, rows)], gss.at[p])

    def fetch(m, c, rows):
        p = lax.rem(c, 2)
        return pltpu.make_async_copy(pq_hbm.at[m, span(c, rows)], bst.at[p, pl.ds(0, rows)], bss.at[p])

    def fetch_w(m):
        p = lax.rem(m, 2)
        return [pltpu.make_async_copy(dgu_hbm.at[m], wgin.at[p], ws.at[p, 0]), pltpu.make_async_copy(hid_hbm.at[m], whin.at[p], ws.at[p, 1])]

    def pieces(n, go):
        def one(c, _):
            go(c)
            return 0

        lax.fori_loop(0, n, one, 0)

    def sent(send, m):
        sized(m, lambda rows, n: pieces(n, lambda c: send(m, c, rows).wait_send()))

    loads = [pltpu.make_async_copy(wg_ref.at[0], wgu.at[:, pl.ds(0, ff)], wsem.at[0])]
    for n, (src, dst) in enumerate(up_parts()):
        loads.append(pltpu.make_async_copy(wu_ref.at[0, :, pl.ds(*src)], wgu.at[:, pl.ds(*dst)], wsem.at[1 + n]))
    loads.append(pltpu.make_async_copy(wd_ref.at[0], wd, wsem.at[3]))

    @pl.when(me == 0)
    def _():
        sized(0, lambda rows, n: pieces(n, lambda c: h_in(0, c, rows).start()))

    for copy in loads:
        copy.start()

    @pl.when(me == 0)
    def _():
        def go(m, _):
            sized(m, lambda rows, n: pieces(n, lambda c: h_in(m, c, rows).start()))
            return 0

        lax.fori_loop(1, micro, go, 0)

    @pl.when(me == last)
    def _():
        def go(m, _):
            sized(m, lambda rows, n: pieces(n, lambda c: d_in(m, c, rows).start()))
            return 0

        lax.fori_loop(0, micro, go, 0)

    barrier = pltpu.get_barrier_semaphore()

    @pl.when(me > 0)
    def _():
        pl.semaphore_signal(barrier, inc=1, device_id={"pp": me - 1})

    @pl.when(me < last)
    def _():
        pl.semaphore_signal(barrier, inc=1, device_id={"pp": me + 1})

    @pl.when((me > 0) & (me < last))
    def _():
        pl.semaphore_wait(barrier, 2)

    @pl.when((me == 0) | (me == last))
    def _():
        pl.semaphore_wait(barrier, 1)

    for copy in loads:
        copy.wait()

    def pairs(a):
        for g0, u0, w in columns(ff):
            if w == TILE:
                g, u = dot(a, wgu[:, g0:g0 + w]), dot(a, wgu[:, u0:u0 + w])
            else:
                gu = dot(a, wgu[:, g0:g0 + 2 * w])
                g, u = gu[:, :w], gu[:, w:]
            yield g0, u0, w, g, u

    def units(a, to, p, rows):
        for g0, u0, w, g, u in pairs(a):
            sig = lax.logistic(g)
            silu = g * sig
            hidf[p, :rows, g0:g0 + w] = (silu * u).astype(BF16)
            to[p, :rows, g0:g0 + w] = u * (sig + silu * (1.0 - sig))
            to[p, :rows, u0:u0 + w] = silu

    def forward(m, settled, rows, n):
        def piece(c):
            r, p = span(c, rows), lax.rem(c, 2)
            h_in(m, c, rows).wait()

            @pl.when(c >= 2)
            def _():
                keep_pq(m, c - 2, rows).wait()
                keep_hid(m, c - 2, rows).wait()

            @pl.when((c < 2) & (settled < m))
            def _():
                sized(m - 1, lambda rows, n: [keep_pq(m - 1, n - 2 + c, rows).wait(), keep_hid(m - 1, n - 2 + c, rows).wait()])

            h = hin[m, r]
            units(normed(h), fst, p, rows)
            hout[lax.rem(m, SLOTS), r] = h + dot(hidf[p, :rows], wd[...]).astype(BF16)
            f_send(m, c, rows).start()
            keep_pq(m, c, rows).start()
            keep_hid(m, c, rows).start()

        pieces(n, piece)

    def settle_f(m):
        sized(m, lambda rows, n: [keep(m, n - k, rows).wait() for k in (2, 1) for keep in (keep_pq, keep_hid)])

    def settle_b(m):
        def go(rows, n):
            for k in (2, 1):
                keep_dgu(m, n - k, rows).wait()

            @pl.when(me == last)
            def _():
                for k in (2, 1):
                    keep_hid(m, n - k, rows).wait()

        sized(m, go)

    def backward(m, settled, more, rows, n):
        def piece(c):
            r, p = span(c, rows), lax.rem(c, 2)

            @pl.when(c >= 2)
            def _():
                keep_dgu(m, c - 2, rows).wait()

            @pl.when((c < 2) & (settled < m))
            def _():
                sized(m - 1, lambda rows, n: keep_dgu(m - 1, n - 2 + c, rows).wait())

            @pl.when(me == last)
            def _():
                h_in(m, c, rows).wait()

                @pl.when(c >= 2)
                def _():
                    keep_hid(m, c - 2, rows).wait()

                @pl.when((c < 2) & (settled < m))
                def _():
                    sized(m - 1, lambda rows, n: keep_hid(m - 1, n - 2 + c, rows).wait())

                units(normed(hin[m, r]), bst, p, rows)
                keep_hid(m, c, rows).start()

            @pl.when(me < last)
            def _():
                fetch(m, c, rows).wait()

            d_in(m, c, rows).wait()
            by_y = din[m, r]
            for g0, u0, w in columns(ff):
                by_z = dot(by_y, wdt[:, g0:g0 + w]).astype(BF16).astype(F32)
                gst[p, :rows, g0:g0 + w] = (by_z * bst[p, :rows, g0:g0 + w]).astype(BF16)
                gst[p, :rows, u0:u0 + w] = (by_z * bst[p, :rows, u0:u0 + w]).astype(BF16)
            by_a = dot(gst[p, :rows, :ff], wgut[:ff]).astype(BF16) + dot(gst[p, :rows, ff:], wgut[ff:]).astype(BF16)
            by_a = by_a.astype(F32)
            wide = hin[m, r].astype(F32)
            scale = scale_of(wide)
            by_scale = jnp.sum(by_a * wide, -1, keepdims=True)
            by_wide = by_a * scale - wide * (by_scale * scale * scale * scale * (1.0 / d))
            bout[lax.rem(m, SLOTS), r] = by_y + by_wide.astype(BF16)

            @pl.when(me > 0)
            def _():
                b_send(m, c, rows).start()

            keep_dgu(m, c, rows).start()

            @pl.when((me < last) & (c + 2 < n))
            def _():
                fetch(m, c + 2, rows).start()

            @pl.when(more & (c + 2 >= n))
            def _():
                sized(m + 1, lambda rows, _: fetch(m + 1, c + 2 - n, rows).start())

        pieces(n, piece)

    def gradients(m):
        p = lax.rem(m, 2)
        dyt[...] = din[m].T
        at[...] = normed(hin[m]).T
        for n in range(0, ff, TILE):
            w = min(TILE, ff - n)
            acc_d[:, n:n + w] += dot(dyt[...], whin[p, :, n:n + w]).astype(BF16).astype(F32)
        for n in range(0, 2 * ff, TILE):
            w = min(TILE, 2 * ff - n)
            acc_gu[:, n:n + w] += dot(at[...], wgin[p, :, n:n + w]).astype(BF16).astype(F32)

    def step(k, carry):
        now, nf, nb, nw, kf, kb, ab, aw = carry
        after = jnp.where(k + 1 < steps, code(k + 1), 0)
        is_f, is_b, is_w = (now == n for n in (1, 2, 3))

        w_next = jnp.where(is_w, jnp.where(aw > nw, nw + 1, nw), nw)
        ask_w = jnp.where(is_w & (aw <= nw), True, (after == 3) & (w_next < nb) & (aw <= w_next))
        b_next = nb
        ask_b = (me < last) & (ab <= nb) & (nb < nf) & (is_b | (after == 2))
        go_f = ((ask_b & (kf <= b_next)) | (is_b & (after == 2) & (me < last) & (nb + 1 < nf) & (kf <= nb + 1))) & (kf < nf)
        go_b = ask_w & (kb <= w_next) & (kb < nb)

        @pl.when(go_f)
        def _():
            settle_f(nf - 1)

        @pl.when(go_b)
        def _():
            settle_b(nb - 1)

        @pl.when(ask_b)
        def _():
            sized(b_next, lambda rows, n: [fetch(b_next, 0, rows).start(), fetch(b_next, 1, rows).start()])

        @pl.when(ask_w)
        def _():
            for copy in fetch_w(w_next):
                copy.start()

        kf, kb = jnp.where(go_f, nf, kf), jnp.where(go_b, nb, kb)
        ab, aw = jnp.where(ask_b, nb + 1, ab), jnp.where(ask_w, w_next + 1, aw)
        more = is_b & (after == 2) & (me < last) & (nb + 1 < nf)

        @pl.when(now == 0)
        def _():
            wdt[...] = wd[...].T
            for n in range(0, 2 * ff, TILE):
                w = min(TILE, 2 * ff - n)
                wgut[n:n + w] = wgu[:, n:n + w].T
            acc_gu[...] = jnp.zeros_like(acc_gu)
            acc_d[...] = jnp.zeros_like(acc_d)

        @pl.when(is_f)
        def _():
            @pl.when(nf >= SLOTS)
            def _():
                sent(f_send, nf - SLOTS)

            sized(nf, lambda rows, n: forward(nf, kf, rows, n))

        @pl.when(is_b)
        def _():
            @pl.when((nb >= SLOTS) & (me > 0))
            def _():
                sent(b_send, nb - SLOTS)

            sized(nb, lambda rows, n: backward(nb, kb, more, rows, n))

        @pl.when(is_w)
        def _():
            for copy in fetch_w(nw):
                copy.wait()
            gradients(nw)

        ab = jnp.where(more, nb + 2, ab)
        kf = jnp.where(is_f, nf, kf)
        kb = jnp.where(is_b, nb, kb)
        one = lambda on: jnp.where(on, 1, 0)
        return after, nf + one(is_f), nb + one(is_b), nw + one(is_w), kf, kb, ab, aw

    zero = jnp.int32(0)
    end = lax.fori_loop(0, steps, step, (code(zero),) + (zero,) * 7)

    @pl.when((me < last) & (end[4] < micro))
    def _():
        settle_f(micro - 1)

    @pl.when(end[5] < micro)
    def _():
        settle_b(micro - 1)

    out_gu, out_d = wgin.at[0], wd
    stores = []
    out_gu[:, :ff] = acc_gu[:, :ff].astype(BF16)
    stores.append(pltpu.make_async_copy(out_gu.at[:, pl.ds(0, ff)], og_ref.at[0], osem.at[0]))
    stores[-1].start()
    out_gu[:, ff:] = acc_gu[:, ff:].astype(BF16)
    for n, (dst, src) in enumerate(up_parts()):
        stores.append(pltpu.make_async_copy(out_gu.at[:, pl.ds(*src)], ou_ref.at[0, :, pl.ds(*dst)], osem.at[1 + n]))
        stores[-1].start()
    out_d[...] = acc_d[...].astype(BF16).T
    stores.append(pltpu.make_async_copy(out_d, od_ref.at[0], osem.at[3]))
    stores[-1].start()

    for m in range(micro - SLOTS, micro):
        @pl.when(me < last)
        def _():
            sent(f_send, m)

        @pl.when(me > 0)
        def _():
            sent(b_send, m)

    for copy in stores:
        copy.wait()


def solution(mesh):
    stages = mesh.shape["pp"]

    def step(x, dy, wg, wu, wd):
        micro, tokens, d = x.shape
        ff = wg.shape[-1]
        orders = ORDER
        if stages != len(ORDER) or micro != ORDER[0].count("F"):
            orders = ["T" + ("" if n == stages - 1 else "F" * micro) + "B" * micro + "W" * micro for n in range(stages)]
        cfg = (micro, tokens, d, ff, stages, orders)
        hbm = pl.BlockSpec(memory_space=pl.ANY)
        flops = 2 * micro * tokens * d * ff * 9
        return pl.pallas_call(
            functools.partial(kernel, cfg),
            out_shape=(
                jax.ShapeDtypeStruct((1, d, ff), BF16),
                jax.ShapeDtypeStruct((1, d, ff), BF16),
                jax.ShapeDtypeStruct((1, ff, d), BF16),
                jax.ShapeDtypeStruct((micro, tokens, 2 * ff), F32),
                jax.ShapeDtypeStruct((micro, tokens, ff), BF16),
                jax.ShapeDtypeStruct((micro, tokens, 2 * ff), BF16),
            ),
            in_specs=[hbm] * 5,
            out_specs=(hbm,) * 6,
            scratch_shapes=[
                pltpu.VMEM((micro, tokens, d), BF16),
                pltpu.VMEM((micro, tokens, d), BF16),
                pltpu.VMEM((d, 2 * ff), BF16),
                pltpu.VMEM((2 * ff, d), BF16),
                pltpu.VMEM((ff, d), BF16),
                pltpu.VMEM((d, ff), BF16),
                pltpu.VMEM((d, 2 * ff), F32),
                pltpu.VMEM((d, ff), F32),
                pltpu.VMEM((SLOTS, tokens, d), BF16),
                pltpu.VMEM((SLOTS, tokens, d), BF16),
                pltpu.VMEM((d, tokens), BF16),
                pltpu.VMEM((d, tokens), BF16),
                pltpu.VMEM((2, tokens // CHUNKS, ff), BF16),
                pltpu.VMEM((2, tokens // CHUNKS, 2 * ff), F32),
                pltpu.VMEM((2, tokens // CHUNKS, 2 * ff), F32),
                pltpu.VMEM((2, tokens // CHUNKS, 2 * ff), BF16),
                pltpu.VMEM((2, tokens, 2 * ff), BF16),
                pltpu.VMEM((2, tokens, ff), BF16),
                pltpu.SemaphoreType.DMA((micro, FINE)),
                pltpu.SemaphoreType.DMA((micro, FINE)),
                pltpu.SemaphoreType.DMA((SLOTS, FINE)),
                pltpu.SemaphoreType.DMA((SLOTS, FINE)),
                pltpu.SemaphoreType.DMA((2,)),
                pltpu.SemaphoreType.DMA((2,)),
                pltpu.SemaphoreType.DMA((2,)),
                pltpu.SemaphoreType.DMA((2,)),
                pltpu.SemaphoreType.DMA((2, 2)),
                pltpu.SemaphoreType.DMA((4,)),
                pltpu.SemaphoreType.DMA((4,)),
            ],
            compiler_params=pltpu.CompilerParams(collective_id=0, has_side_effects=True, vmem_limit_bytes=67_000_000),
            cost_estimate=pl.CostEstimate(flops=flops, bytes_accessed=40_000_000, transcendentals=0),
            name="pipeline",
        )(x, dy, wg, wu, wd)[:3]

    return jax.shard_map(
        step,
        mesh=mesh,
        in_specs=(P("rep", None, None),) * 2 + (P("pp", None, None),) * 3,
        out_specs=(P(("rep", "pp"), None, None),) * 3,
        check_vma=False,
    )
```

time: 244 us -> 203 us (0.83)
  Pallas kernels: 238 us -> 196 us
    pallas_call x1, Pallas kernels: 238 us -> 196 us  [step(): pl.pallas_call(functools.partial(kernel, cfg), out_shape=(jax.ShapeDtypeS...]
where the time goes in v2:
time: 203 us
  Pallas kernels  196 us (97%)
  local copies, waits for them, and re-layouts  5.66 us (3%)
    pallas_call x1, Pallas kernels, step(): pl.pallas_call(functools.partial(kernel, cfg), out_shape=(jax.ShapeDtypeS...  196 us
    unnamed x7, local copies, waits for them, and re-layouts  5.66 us

profile of v2, /device:TPU:2, one launch (start us, length us, event | category | flops | bytes accessed | tf_op | source)
XLA Modules:
  0.0 202.6 jit_solution(13153983949861073865)
XLA Ops:
  0.6 196.2 %pipeline.1 = (bf16[1,512,1408]{2,1,0:T(8,128)(2,1)}, bf16[1,512,1408]{2,1,0:T(8,128)(2,1)}, bf16[1,1408,512]{2,1,0:T(8,128)(2,1)}, f32[16,512,2816]{2,1,0:T(8,1...) custom-call(bf16[16,512,512]{2,1,0:T(8,128)(2,1)} %x_ref.1, bf16[16,512,512]{2,1,0:T(8,128)(2,1)} %dy_ref.1, ...), custom_call_target="tpu_custom_call" | custom-call | flops 106300440576 | bytes 40000000 | tf_op jit(solution)/shard_map/pipeline/pallas_call | solution.py:441
  196.9 0.0 copy-start.1
  196.9 2.7 %copy.11 = bf16[1,512,1408]{2,1,0:T(8,128)(2,1)} copy(bf16[1,512,1408]{2,1,0:T(8,128)(2,1)} %get-tuple-element.12) | data formatting | bytes 2883584
  199.6 0.0 copy-done.1
  199.6 0.0 copy-start
  199.6 1.1 copy.12
  200.7 0.8 copy-done
  201.5 1.1 copy.13
Async XLA Ops:
  196.9 2.7 %copy-start.1 = (bf16[1,512,1408]{2,1,0:T(8,128)(2,1)S(1)}, bf16[1,512,1408]{2,1,0:T(8,128)(2,1)}, u32[]{:S(2)}) copy-start(bf16[1,512,1408]{2,1,0:T(8,128)(2,1)} %get-tuple-element.13) | copy-start | bytes 4325380
  199.6 1.9 copy-start

commit v3 on v2

--- a/solution.py
+++ b/solution.py
@@ -12,21 +12,24 @@
 FIRST, FINAL = 1, 1
 SLOTS = 2
 ORDER = (
-    "FTFFFFFFFFFFFFFBFBFWBBWBWWBBWBWBWBWBWBWBWBWWBBWWW",
-    "TFFFFFFFFFFFFFBFBFWBFBWBWWBBWBWBWBWBWBWBWBWWBBWWW",
-    "TFFFFFFBFFFFBFFWFBFBFBFBWBWBWBWBWBWBWBWBWWBBWWWWW",
-    "TFFFFFBFFFFBFWFFBFBFBFBFBWBWBWBWBWBWBWBWWBBWWWWWW",
-    "TFFFBFFFBFWFBFFBFBFBFBFBFBFBBWWBWBWBWWBBWWWWWWWWW",
-    "TFFBFFFBFWBFFBFBFBFBFBFBFBFBFBWBWBWWBBWWWWWWWWWWW",
-    "TFBFBFWFBFWBFBFBFBFBFBFBFBFBFBFBFBBWWWWWWWWWWWWWW",
-    "TBBBWBBWBBWBBWBBWBBWBBBWWWWWWWWWW",
+    "FTFFFFFFFFFFFFFBFFBWBWBWBWBWBWBWBWBWBWBWBWBWBWBWW",
+    "TFFFFFFFFFFFFFBFMFBWBWBWBWBWBWBWBWBWBWBWBWBWBWWW",
+    "TFFFFFFFFFFBFMMMMFBWBWBWBWBWBWBWBWBWBWBWWWWWW",
+    "TFFFFFFFFFBFMMMMMFBWBWBWBWBWBWBWBWBWBWWWWWWW",
+    "TFFFFFFBFMMMMMMMMFBWBWBWBWBWBWBWWWWWWWWWW",
+    "TFFFFFBFMMMMMMMMMFBWBWBWBWBWBWWWWWWWWWWW",
+    "TFFBFMMMMMMMMMMMMFBWBWBWWWWWWWWWWWWWW",
+    "TBBBWBBWBBWBBWBBWBBWBBWBWWWWWWWWW",
 )
 TILE = 256
 
 
+SPAN = 9
+
+
 def packed(order):
-    codes = ["TFBW".index(step) for step in order]
-    return [sum(code * 4**n for n, code in enumerate(codes[k:k + 15])) for k in range(0, len(codes), 15)]
+    codes = ["TFBWM".index(step) for step in order]
+    return [sum(code * 8**n for n, code in enumerate(codes[k:k + SPAN + 1])) for k in range(0, len(codes), SPAN)]
 
 
 def dot(a, b):
@@ -65,9 +68,8 @@
     words = [packed(order) for order in orders]
     steps = by_stage([len(order) for order in orders])
 
-    def code(k):
-        word = sum(jnp.where(k // 15 == j, by_stage([w[j] if j < len(w) else 0 for w in words]), 0) for j in range(max(map(len, words))))
-        return (word // sum(jnp.where(k % 15 == j, 4**j, 0) for j in range(15))) % 4
+    def word(j):
+        return sum(jnp.where(j == k, by_stage([w[k] if k < len(w) else 0 for w in words]), 0) for k in range(max(map(len, words))))
 
     def is_fine(m):
         return (m < FIRST) | (m >= micro - FINAL)
@@ -230,7 +232,7 @@
             keep_pq(m, c, rows).start()
             keep_hid(m, c, rows).start()
 
-        pieces(n, piece)
+        return piece
 
     def settle_f(m):
         sized(m, lambda rows, n: [keep(m, n - k, rows).wait() for k in (2, 1) for keep in (keep_pq, keep_hid)])
@@ -279,21 +281,29 @@
                 fetch(m, c, rows).wait()
 
             d_in(m, c, rows).wait()
-            by_y = din[m, r]
-            for g0, u0, w in columns(ff):
-                by_z = dot(by_y, wdt[:, g0:g0 + w]).astype(BF16).astype(F32)
-                gst[p, :rows, g0:g0 + w] = (by_z * bst[p, :rows, g0:g0 + w]).astype(BF16)
-                gst[p, :rows, u0:u0 + w] = (by_z * bst[p, :rows, u0:u0 + w]).astype(BF16)
-            by_a = dot(gst[p, :rows, :ff], wgut[:ff]).astype(BF16) + dot(gst[p, :rows, ff:], wgut[ff:]).astype(BF16)
-            by_a = by_a.astype(F32)
-            wide = hin[m, r].astype(F32)
-            scale = scale_of(wide)
-            by_scale = jnp.sum(by_a * wide, -1, keepdims=True)
-            by_wide = by_a * scale - wide * (by_scale * scale * scale * scale * (1.0 / d))
-            bout[lax.rem(m, SLOTS), r] = by_y + by_wide.astype(BF16)
+
+            def units_back():
+                by_y = din[m, r]
+                for g0, u0, w in columns(ff):
+                    by_z = dot(by_y, wdt[:, g0:g0 + w]).astype(BF16).astype(F32)
+                    gst[p, :rows, g0:g0 + w] = (by_z * bst[p, :rows, g0:g0 + w]).astype(BF16)
+                    gst[p, :rows, u0:u0 + w] = (by_z * bst[p, :rows, u0:u0 + w]).astype(BF16)
+                return by_y
+
+            @pl.when(me == 0)
+            def _():
+                units_back()
 
             @pl.when(me > 0)
             def _():
+                by_y = units_back()
+                by_a = dot(gst[p, :rows, :ff], wgut[:ff]).astype(BF16) + dot(gst[p, :rows, ff:], wgut[ff:]).astype(BF16)
+                by_a = by_a.astype(F32)
+                wide = hin[m, r].astype(F32)
+                scale = scale_of(wide)
+                by_scale = jnp.sum(by_a * wide, -1, keepdims=True)
+                by_wide = by_a * scale - wide * (by_scale * scale * scale * scale * (1.0 / d))
+                bout[lax.rem(m, SLOTS), r] = by_y + by_wide.astype(BF16)
                 b_send(m, c, rows).start()
 
             keep_dgu(m, c, rows).start()
@@ -306,12 +316,15 @@
             def _():
                 sized(m + 1, lambda rows, _: fetch(m + 1, c + 2 - n, rows).start())
 
-        pieces(n, piece)
+        return piece
+
+    def transposed(m):
+        dyt[...] = din[m].T
+        at[...] = normed(hin[m]).T
 
     def gradients(m):
         p = lax.rem(m, 2)
-        dyt[...] = din[m].T
-        at[...] = normed(hin[m]).T
+        transposed(m)
         for n in range(0, ff, TILE):
             w = min(TILE, ff - n)
             acc_d[:, n:n + w] += dot(dyt[...], whin[p, :, n:n + w]).astype(BF16).astype(F32)
@@ -319,16 +332,40 @@
             w = min(TILE, 2 * ff - n)
             acc_gu[:, n:n + w] += dot(at[...], wgin[p, :, n:n + w]).astype(BF16).astype(F32)
 
+    final = (micro - 1) % 2
+    out_gu, out_d = wgin.at[1 - final], wd
+    stores = [pltpu.make_async_copy(out_d, od_ref.at[0], osem.at[0]), pltpu.make_async_copy(out_gu.at[:, pl.ds(0, ff)], og_ref.at[0], osem.at[1])]
+    for n, (dst, src) in enumerate(up_parts()):
+        stores.append(pltpu.make_async_copy(out_gu.at[:, pl.ds(*src)], ou_ref.at[0, :, pl.ds(*dst)], osem.at[2 + n]))
+
+    def gradients_last():
+        transposed(micro - 1)
+        for n in range(0, ff, TILE):
+            w = min(TILE, ff - n)
+            total = acc_d[:, n:n + w] + dot(dyt[...], whin[final, :, n:n + w]).astype(BF16).astype(F32)
+            out_d[n:n + w] = total.astype(BF16).T
+        stores[0].start()
+        for n in range(0, 2 * ff, TILE):
+            w = min(TILE, 2 * ff - n)
+            total = acc_gu[:, n:n + w] + dot(at[...], wgin[final, :, n:n + w]).astype(BF16).astype(F32)
+            out_gu[:, n:n + w] = total.astype(BF16)
+            if n < ff <= n + w:
+                stores[1].start()
+        for copy in stores[2:]:
+            copy.start()
+
     def step(k, carry):
-        now, nf, nb, nw, kf, kb, ab, aw = carry
-        after = jnp.where(k + 1 < steps, code(k + 1), 0)
-        is_f, is_b, is_w = (now == n for n in (1, 2, 3))
+        rest, nf, nb, nw, kf, kb, ab, aw = carry
+        now, rest = lax.rem(rest, 8), lax.div(rest, 8)
+        after = lax.rem(rest, 8)
+        after_b = (after == 2) | (after == 4)
+        is_f, is_b, is_w = (now == 1) | (now == 4), (now == 2) | (now == 4), now == 3
 
         w_next = jnp.where(is_w, jnp.where(aw > nw, nw + 1, nw), nw)
         ask_w = jnp.where(is_w & (aw <= nw), True, (after == 3) & (w_next < nb) & (aw <= w_next))
         b_next = nb
-        ask_b = (me < last) & (ab <= nb) & (nb < nf) & (is_b | (after == 2))
-        go_f = ((ask_b & (kf <= b_next)) | (is_b & (after == 2) & (me < last) & (nb + 1 < nf) & (kf <= nb + 1))) & (kf < nf)
+        ask_b = (me < last) & (ab <= nb) & (nb < nf) & (is_b | after_b)
+        go_f = ((ask_b & (kf <= b_next)) | (is_b & after_b & (me < last) & (nb + 1 < nf) & (kf <= nb + 1))) & (kf < nf)
         go_b = ask_w & (kb <= w_next) & (kb < nb)
 
         @pl.when(go_f)
@@ -350,7 +387,7 @@
 
         kf, kb = jnp.where(go_f, nf, kf), jnp.where(go_b, nb, kb)
         ab, aw = jnp.where(ask_b, nb + 1, ab), jnp.where(ask_w, w_next + 1, aw)
-        more = is_b & (after == 2) & (me < last) & (nb + 1 < nf)
+        more = is_b & after_b & (me < last) & (nb + 1 < nf)
 
         @pl.when(now == 0)
         def _():
@@ -361,36 +398,57 @@
             acc_gu[...] = jnp.zeros_like(acc_gu)
             acc_d[...] = jnp.zeros_like(acc_d)
 
-        @pl.when(is_f)
-        def _():
-            @pl.when(nf >= SLOTS)
-            def _():
-                sent(f_send, nf - SLOTS)
-
-            sized(nf, lambda rows, n: forward(nf, kf, rows, n))
-
-        @pl.when(is_b)
-        def _():
-            @pl.when((nb >= SLOTS) & (me > 0))
-            def _():
-                sent(b_send, nb - SLOTS)
-
-            sized(nb, lambda rows, n: backward(nb, kb, more, rows, n))
+        @pl.when(is_f & (nf >= SLOTS))
+        def _():
+            sent(f_send, nf - SLOTS)
+
+        @pl.when(is_b & (nb >= SLOTS) & (me > 0))
+        def _():
+            sent(b_send, nb - SLOTS)
+
+        def work(rows, n):
+            ahead, back = forward(nf, kf, rows, n), backward(nb, kb, more, rows, n)
+
+            def piece(c):
+                @pl.when(is_f)
+                def _():
+                    ahead(c)
+
+                @pl.when(is_b)
+                def _():
+                    back(c)
+
+            pieces(n, piece)
+
+        @pl.when(is_f | is_b)
+        def _():
+            sized(jnp.where(is_f, nf, nb), work)
 
         @pl.when(is_w)
         def _():
             for copy in fetch_w(nw):
                 copy.wait()
-            gradients(nw)
+
+            @pl.when(nw < micro - 1)
+            def _():
+                gradients(nw)
+
+            @pl.when(nw == micro - 1)
+            def _():
+                gradients_last()
 
         ab = jnp.where(more, nb + 2, ab)
         kf = jnp.where(is_f, nf, kf)
         kb = jnp.where(is_b, nb, kb)
         one = lambda on: jnp.where(on, 1, 0)
-        return after, nf + one(is_f), nb + one(is_b), nw + one(is_w), kf, kb, ab, aw
+        return rest, nf + one(is_f), nb + one(is_b), nw + one(is_w), kf, kb, ab, aw
 
     zero = jnp.int32(0)
-    end = lax.fori_loop(0, steps, step, (code(zero),) + (zero,) * 7)
+
+    def steps_of(j, carry):
+        return lax.fori_loop(0, jnp.minimum(SPAN, steps - SPAN * j), step, (word(j),) + carry)[1:]
+
+    end = (zero,) + lax.fori_loop(0, (steps + SPAN - 1) // SPAN, steps_of, (zero,) * 7)
 
     @pl.when((me < last) & (end[4] < micro))
     def _():
@@ -399,19 +457,6 @@
     @pl.when(end[5] < micro)
     def _():
         settle_b(micro - 1)
-
-    out_gu, out_d = wgin.at[0], wd
-    stores = []
-    out_gu[:, :ff] = acc_gu[:, :ff].astype(BF16)
-    stores.append(pltpu.make_async_copy(out_gu.at[:, pl.ds(0, ff)], og_ref.at[0], osem.at[0]))
-    stores[-1].start()
-    out_gu[:, ff:] = acc_gu[:, ff:].astype(BF16)
-    for n, (dst, src) in enumerate(up_parts()):
-        stores.append(pltpu.make_async_copy(out_gu.at[:, pl.ds(*src)], ou_ref.at[0, :, pl.ds(*dst)], osem.at[1 + n]))
-        stores[-1].start()
-    out_d[...] = acc_d[...].astype(BF16).T
-    stores.append(pltpu.make_async_copy(out_d, od_ref.at[0], osem.at[3]))
-    stores[-1].start()
 
     for m in range(micro - SLOTS, micro):
         @pl.when(me < last)
@@ -424,6 +469,27 @@
 
     for copy in stores:
         copy.wait()
+
+
+PARTS = 4
+
+
+def hand_on(*refs):
+    ins, outs, held, in_sem, out_sem = refs[:3], refs[3:6], refs[6:9], refs[9], refs[10]
+    moves = []
+    for n in range(3):
+        rows = ins[n].shape[1] // PARTS
+        for k in range(PARTS):
+            r = pl.ds(k * rows, rows)
+            moves.append((pltpu.make_async_copy(ins[n].at[:, r], held[n].at[:, r], in_sem.at[n, k]),
+                          pltpu.make_async_copy(held[n].at[:, r], outs[n].at[:, r], out_sem.at[n, k])))
+    for take, _ in moves:
+        take.start()
+    for take, put in moves:
+        take.wait()
+        put.start()
+    for _, put in moves:
+        put.wait()
 
 
 def solution(mesh):
@@ -433,12 +499,12 @@
         micro, tokens, d = x.shape
         ff = wg.shape[-1]
         orders = ORDER
-        if stages != len(ORDER) or micro != ORDER[0].count("F"):
+        if stages != len(ORDER) or micro != ORDER[0].count("F") + ORDER[0].count("M"):
             orders = ["T" + ("" if n == stages - 1 else "F" * micro) + "B" * micro + "W" * micro for n in range(stages)]
         cfg = (micro, tokens, d, ff, stages, orders)
         hbm = pl.BlockSpec(memory_space=pl.ANY)
         flops = 2 * micro * tokens * d * ff * 9
-        return pl.pallas_call(
+        grads = pl.pallas_call(
             functools.partial(kernel, cfg),
             out_shape=(
                 jax.ShapeDtypeStruct((1, d, ff), BF16),
@@ -485,6 +551,15 @@
             cost_estimate=pl.CostEstimate(flops=flops, bytes_accessed=40_000_000, transcendentals=0),
             name="pipeline",
         )(x, dy, wg, wu, wd)[:3]
+        return pl.pallas_call(
+            hand_on,
+            out_shape=tuple(jax.ShapeDtypeStruct(g.shape, g.dtype) for g in grads),
+            in_specs=[hbm] * 3,
+            out_specs=(hbm,) * 3,
+            scratch_shapes=[pltpu.VMEM(g.shape, g.dtype) for g in grads] + [pltpu.SemaphoreType.DMA((3, PARTS))] * 2,
+            compiler_params=pltpu.CompilerParams(vmem_limit_bytes=60_000_000),
+            name="hand_on",
+        )(*grads)
 
     return jax.shard_map(
         step,

time: 203 us -> 195 us (0.961)
  local copies, waits for them, and re-layouts: 5.66 us -> 0 us
    pallas_call x1, Pallas kernels: 196 us -> 190 us  [step(): pl.pallas_call(functools.partial(kernel, cfg), out_shape=(jax.ShapeDtypeS...]
    unnamed x7 -> x0, local copies, waits for them, and re-layouts: 5.66 us -> none
    pallas_call x0 -> x1, Pallas kernels: none -> 3.86 us  [step(): pl.pallas_call(hand_on, out_shape=tuple((jax.ShapeDtypeStruct(g.shape, g....]
where the time goes in v3:
time: 195 us; the launch traced here: 194 us
  Pallas kernels  194 us (99%)
    pallas_call x1, Pallas kernels, step(): pl.pallas_call(functools.partial(kernel, cfg), out_shape=(jax.ShapeDtypeS...  190 us

profile of v3, /device:TPU:2, one launch (start us, length us, event | category | flops | bytes accessed | tf_op | source)
XLA Modules:
  0.0 194.2 jit_solution(12935422136618677468)
XLA Ops:
  0.6 189.8 %pipeline.1 = (bf16[1,512,1408]{2,1,0:T(8,128)(2,1)}, bf16[1,512,1408]{2,1,0:T(8,128)(2,1)}, bf16[1,1408,512]{2,1,0:T(8,128)(2,1)}, f32[16,512,2816]{2,1,0:T(8,1...) custom-call(bf16[16,512,512]{2,1,0:T(8,128)(2,1)} %x_ref.1, bf16[16,512,512]{2,1,0:T(8,128)(2,1)} %dy_ref.1, ...), custom_call_target="tpu_custom_call" | custom-call | flops 106300440576 | bytes 40000000 | tf_op jit(solution)/shard_map/pipeline/pallas_call | solution.py:507
  190.4 3.9 %hand_on.1 = (bf16[1,512,1408]{2,1,0:T(8,128)(2,1)}, bf16[1,512,1408]{2,1,0:T(8,128)(2,1)}, bf16[1,1408,512]{2,1,0:T(8,128)(2,1)}) custom-call(bf16[1,512,1408]{2,1,0:T(8,128)(2,1)} %get-tuple-element.6.refs_0_, bf16[1,512,1408]{2,1,0:T(8,128)(2,1)} %get-tuple-element.7.refs_1_, bf16[1,1408,512]{2,1,0:T(8,128)(2,1)} %get-tuple-element.8.refs_2_), custom_call_target="tpu_custom_call" | custom-call | tf_op jit(solution)/shard_map/hand_on/pallas_call | solution.py:554
